TPU v7x, 256 devices: a whole 4x4x8 slice. The times are simulated.
256 devices in a mesh: ctx: 8 (over z), vocab: 32 (over y, x, core).
Axes of the slice: x: 4, y: 4, z: 8, core: 2. Of those that a mesh axis runs over, the one named last changes fastest.
Arguments:
- hidden: bfloat16 [16, 128, 4096], P(None, 'ctx', 'vocab'), may hold values from -6 to 6
- head_weight: bfloat16 [4096, 128256], P(None, ('ctx', 'vocab')), may hold values from -0.09375 to 0.09375
- token_ids: int32 [16, 128], P(None, 'ctx'), may hold values from 0 to 128255
- response_mask: int32 [16, 128], P(None, 'ctx'), may hold values 0 or 1
- pair_order: int32 [16], replicated, may hold values from 0 to 15, each once
- frozen_logprob: float32 [16], replicated, may hold values from -40 to 40
Outputs:
- pair_loss: float32 [], replicated
- margins: float32 [8], replicated
- head_grad: bfloat16 [4096, 128256], P(None, ('ctx', 'vocab'))
- spread_grad: bfloat16 [4096, 128256], P(None, ('ctx', 'vocab'))
Inputs may be any that keep to these rules, and one draw needn't show every extreme that they name: `token_ids`: token ids lie in 0 to 128255. `response_mask`: mask entries are 0 or 1. pair_order names every sequence exactly once; entry p is the chosen sequence of pair p and entry 8 + p the rejected one.
All inputs are finite; a program needn't handle non-finite values.
Results may differ from a plain program's by a relative error of at most 0.0015.
Values may be sent and summed in bfloat16 or wider, within the bound.
A program may use at most 128 MiB of HBM per device.

v0:
```python
import jax
import jax.numpy as jnp
from jax import lax
from jax.sharding import Mesh
from jax.sharding import PartitionSpec as P

V = 128256
VOCAB = ("vocab_0", "vocab_1", "vocab_2")
CTX_VOCAB = ("ctx", "vocab_0", "vocab_1", "vocab_2")
strength = 0.1
loss_scale = 256.0


def laid_out(pieces, dim):
    pieces = jnp.moveaxis(pieces, 0, dim)
    lengths = pieces.shape
    return pieces.reshape(*lengths[:dim], lengths[dim] * lengths[dim + 1], *lengths[dim + 2 :])


def gather_packed(arrays, axis, dims):
    flat = jnp.concatenate([a.reshape(-1) for a in arrays])
    lines, at, finished = (lax.all_gather(flat, axis), 0, [])
    for a, dim in zip(arrays, dims):
        pieces = lines[:, at : at + a.size].reshape(-1, *a.shape)
        finished.append(laid_out(pieces, dim))
        at += a.size
    return tuple(finished)


def by_axis(shard, axes):
    for axis in axes:
        shard = lax.pmax(shard, axis)
    return shard


def by_axis_2(shard, axes):
    for axis in axes:
        shard = lax.psum(shard, axis)
    return shard


def contract_rows(block_rows, both_logits):
    return lax.dot_general(
        block_rows, both_logits, (((0,), (0,)), ((), ())), preferred_element_type=jnp.float32
    )


def shards(hidden, head_weight, token_ids, response_mask, pair_order, frozen_logprob):
    seq_rows = lax.all_gather(hidden, "ctx", axis=1, tiled=True)
    ids_all, mask_all = gather_packed((token_ids, response_mask), "ctx", (1, 1))
    token_rows = seq_rows.reshape(seq_rows.shape[0] * seq_rows.shape[1], seq_rows.shape[2])
    shard_width = head_weight.shape[1]
    whole_rows = lax.all_gather(token_rows, VOCAB, axis=1, tiled=True)
    logits = jnp.dot(whole_rows, head_weight, preferred_element_type=jnp.float32)
    offset = lax.axis_index(CTX_VOCAB) * shard_width
    local_ids = ids_all.reshape(-1) - offset
    columns = jnp.arange(shard_width).astype(jnp.int32)
    onehot = (columns[None, :] == local_ids[:, None]).astype(jnp.float32)
    picked_part = jnp.sum(onehot * logits, axis=1)
    peak_part = jnp.max(logits, axis=1)
    row_peak = by_axis(peak_part, CTX_VOCAB)
    exp_sums = jnp.sum(jnp.exp(logits - row_peak[:, None]), axis=1)
    sum_total, picked = (by_axis_2(exp_sums, CTX_VOCAB), by_axis_2(picked_part, CTX_VOCAB))
    log_norm = row_peak + jnp.log(sum_total)
    mask_flat = mask_all.reshape(-1).astype(jnp.float32)
    seq_count = ids_all.shape[0]
    policy = jnp.sum(((picked - log_norm) * mask_flat).reshape(seq_count, ids_all.shape[1]), axis=1)
    log_ratio = policy - frozen_logprob
    pair_count = pair_order.shape[0] // 2
    chosen = pair_order[:pair_count]
    rejected = pair_order[pair_count:]
    margins = strength * (log_ratio[chosen] - log_ratio[rejected])
    pair_loss = jnp.mean(jax.nn.softplus(-margins))
    weight = -loss_scale * strength * jax.nn.sigmoid(-margins) / pair_count
    seq_coef = jnp.zeros((seq_count,), jnp.float32).at[chosen].set(weight).at[rejected].set(-weight)
    token_coef = (seq_coef[:, None] * mask_all.astype(jnp.float32)).reshape(-1)
    probabilities = jnp.exp(logits - log_norm[:, None])
    grad_logits = (token_coef[:, None] * (onehot - probabilities)).astype(jnp.bfloat16)
    spread_logits = (V / 64.0 * token_coef[:, None] * probabilities).astype(jnp.bfloat16)
    both_logits = jnp.concatenate([grad_logits, spread_logits], axis=1)
    both_grads = contract_rows(whole_rows, both_logits)
    head_grad = both_grads[:, :shard_width].astype(jnp.bfloat16)
    spread_grad = both_grads[:, shard_width:].astype(jnp.bfloat16)
    return (pair_loss, margins, head_grad, spread_grad)


def solution(mesh):
    split = Mesh(
        mesh.devices.reshape(mesh.shape["ctx"], 4, 4, 2), ("ctx", "vocab_0", "vocab_1", "vocab_2")
    )
    placed = (P(None, "ctx", VOCAB), P(None, CTX_VOCAB), P(None, "ctx"), P(None, "ctx"), P(), P())
    return jax.shard_map(
        shards,
        mesh=split,
        in_specs=placed,
        out_specs=(P(), P(), P(None, CTX_VOCAB), P(None, CTX_VOCAB)),
        check_vma=False,
    )
```

profile of v0, /device:TPU:1, one launch (start us, length us, event | category | flops | bytes accessed | tf_op | source)
XLA Modules:
  0.0 282.0 jit_solution(17380326910799111413)
XLA Ops:
  7.2 0.0 all-gather.4.cloned.1.call-start
  7.2 26.5 %all_gather.14 = bf16[16,128,128]{2,1,0:T(8,128)(2,1)} all-gather(bf16[16,16,128]{2,1,0:T(8,128)(2,1)} %param.6), channel_id=1, replica_groups=mesh['ctx'=8,'vocab_0'=4,'vocab_1'=4,'vocab_2'=2] {'ctx'}, dimensions={1}, use_global_device_ids=true | all-gather | bytes 589824 | tf_op jit(solution)/shard_map/all_gather | solution.py:49
  33.7 0.0 all-gather.4.cloned.1.call-update
  33.7 0.8 reshape.60
  34.5 0.8 reshape.61
  35.3 16.1 %all-gather.1 = s32[8,1,512]{2,1,0:T(1,128)S(1)} all-gather(s32[1,1,512]{2,1,0:T(1,128)S(1)} %bitcast.21), channel_id=2, replica_groups=mesh['ctx'=8,'vocab_0'=4,'vocab_1'=4,'vocab_2'=2] {'ctx'}, dimensions={0}, use_global_device_ids=true | all-gather | bytes 18432 | tf_op jit(solution)/shard_map/all_gather | solution.py:22
  51.4 0.1 sub.49
  51.5 0.1 sub.51
  51.6 0.1 convert_element_type.33
  51.7 0.1 convert_element_type.35
  51.8 0.8 compare_select_fusion.1
  52.6 71.6 %all-gather.4.cloned.1.call-done = bf16[2048,4096]{1,0:T(8,128)(2,1)} async-done(((bf16[2048,128]{1,0:T(8,128)(2,1)}), bf16[2048,4096]{1,0:T(8,128)(2,1)}) %all-gather.4.cloned.1.call-update) | async-done | bytes 16777232 | tf_op jit(solution)/shard_map/all_gather | solution.py:53
  124.2 14.8 %fusion.9 = (f32[2048]{0:T(1024)S(1)}, f32[2048,501]{0,1:T(8,128)}) fusion(bf16[2048,4096]{1,0:T(8,128)(2,1)} %all-gather.4.cloned.1.call-done, bf16[4096,501]{0,1:T(8,128)(2,1)} %param.7), kind=kOutput, calls=%fused_computation.35 | convolution fusion | flops 8406409216 | bytes 24993792 | tf_op jit(solution)/shard_map/dot_general | solution.py:54
  139.0 0.0 copy-start.1
  139.0 14.1 %pmax.28 = f32[2048]{0:T(1024)S(1)} all-reduce(f32[2048]{0:T(1024)S(1)} %get-tuple-element.29), channel_id=1, replica_groups=mesh['ctx'=8,'vocab_0'=4,'vocab_1'=4,'vocab_2'=2] {'ctx'}, use_global_device_ids=true, to_apply=%region_6.0 | all-reduce | flops 2048 | bytes 16384 | tf_op jit(solution)/shard_map/pmax | solution.py:32
  153.1 8.2 %pmax.29 = f32[2048]{0:T(1024)S(1)} all-reduce(f32[2048]{0:T(1024)S(1)} %pmax.28), channel_id=1, replica_groups=mesh['ctx'=8,'vocab_0'=4,'vocab_1'=4,'vocab_2'=2] {'vocab_0'}, use_global_device_ids=true, to_apply=%region_7.0 | all-reduce | flops 2048 | bytes 16384 | tf_op jit(solution)/shard_map/pmax | solution.py:32
  161.3 7.4 %pmax.30 = f32[2048]{0:T(1024)S(1)} all-reduce(f32[2048]{0:T(1024)S(1)} %pmax.29), channel_id=1, replica_groups=mesh['ctx'=8,'vocab_0'=4,'vocab_1'=4,'vocab_2'=2] {'vocab_1'}, use_global_device_ids=true, to_apply=%region_8.0 | all-reduce | flops 2048 | bytes 16384 | tf_op jit(solution)/shard_map/pmax | solution.py:32
  168.7 10.1 %pmax.31 = f32[2048]{0:T(1024)S(1)} all-reduce(f32[2048]{0:T(1024)S(1)} %pmax.30), channel_id=1, replica_groups=mesh['ctx'=8,'vocab_0'=4,'vocab_1'=4,'vocab_2'=2] {'vocab_2'}, use_global_device_ids=true, to_apply=%region_9.0 | all-reduce | flops 2048 | bytes 16384 | tf_op jit(solution)/shard_map/pmax | solution.py:32
  178.8 3.3 %exponential_reduce_fusion = (f32[2048]{0:T(1024)S(1)}, f32[2048]{0:T(1024)S(1)}) fusion(f32[2048,501]{0,1:T(8,128)} %get-tuple-element.30, f32[2048]{0:T(1024)S(1)} %pmax.31, s32[2048]{0:T(1024)S(1)} %sub.51), kind=kLoop, calls=%fused_computation.11 | loop fusion | flops 5126144 | bytes 4136960 | tf_op jit(solution)/shard_map/reduce_sum | solution.py:62
  182.1 20.5 %all-reduce = (f32[2048]{0:T(1024)S(1)}, f32[2048]{0:T(1024)S(1)}) all-reduce(f32[2048]{0:T(1024)S(1)} %get-tuple-element.5, f32[2048]{0:T(1024)S(1)} %get-tuple-element.4), channel_id=1, replica_groups=mesh['ctx'=8,'vocab_0'=4,'vocab_1'=4,'vocab_2'=2] {'ctx'}, use_global_device_ids=true, to_apply=%region_1.0 | all-reduce | flops 4096 | bytes 32768 | tf_op jit(solution)/shard_map/psum | solution.py:38
  202.6 10.8 %all-reduce.2 = (f32[2048]{0:T(1024)S(1)}, f32[2048]{0:T(1024)S(1)}) all-reduce(f32[2048]{0:T(1024)S(1)} %get-tuple-element.6, f32[2048]{0:T(1024)S(1)} %get-tuple-element.7), channel_id=1, replica_groups=mesh['ctx'=8,'vocab_0'=4,'vocab_1'=4,'vocab_2'=2] {'vocab_0'}, use_global_device_ids=true, to_apply=%region_2.0 | all-reduce | flops 4096 | bytes 32768 | tf_op jit(solution)/shard_map/psum | solution.py:38
  213.4 10.9 %all-reduce.1 = (f32[2048]{0:T(1024)S(1)}, f32[2048]{0:T(1024)S(1)}) all-reduce(f32[2048]{0:T(1024)S(1)} %get-tuple-element.10, f32[2048]{0:T(1024)S(1)} %get-tuple-element.11), channel_id=1, replica_groups=mesh['ctx'=8,'vocab_0'=4,'vocab_1'=4,'vocab_2'=2] {'vocab_1'}, use_global_device_ids=true, to_apply=%region_3.0 | all-reduce | flops 4096 | bytes 32768 | tf_op jit(solution)/shard_map/psum | solution.py:38
  224.3 17.9 %all-reduce.3 = (f32[2048]{0:T(1024)S(1)}, f32[2048]{0:T(1024)S(1)}) all-reduce(f32[2048]{0:T(1024)S(1)} %get-tuple-element.8, f32[2048]{0:T(1024)S(1)} %get-tuple-element.9), channel_id=1, replica_groups=mesh['ctx'=8,'vocab_0'=4,'vocab_1'=4,'vocab_2'=2] {'vocab_2'}, use_global_device_ids=true, to_apply=%region_4.0 | all-reduce | flops 4096 | bytes 32768 | tf_op jit(solution)/shard_map/psum | solution.py:38
  242.2 0.1 bitcast_reduce_fusion
  242.3 0.0 copy-done.1
  242.3 0.6 gather_fusion.1
  243.0 0.6 gather_fusion
  243.6 0.0 copy-start
  243.7 0.6 scatter_custom_fusion
  244.3 0.8 scatter_fusion
  245.1 0.1 broadcast_multiply_fusion
  245.1 3.5 %multiply_convert_fusion.1 = (bf16[2048,501]{0,1:T(8,128)(2,1)S(1)}, bf16[2048,501]{0,1:T(8,128)(2,1)S(1)}) fusion(f32[2048,501]{0,1:T(8,128)} %get-tuple-element.30, f32[2048]{0:T(1024)S(1)} %get-tuple-element.20, f32[2048]{0:T(1024)S(1)} %get-tuple-element.15, s32[2048]{0:T(1024)S(1)} %sub.51, f32[2048]{0:T(1024)S(1)} %get-tuple-element.14), kind=kLoop, calls=%fused_computation.9 | loop fusion | flops 8208384 | bytes 8241152 | tf_op jit(solution)/shard_map/convert_element_type | solution.py:78
  248.7 20.1 %convert_bitcast_fusion = bf16[4096,1002]{0,1:T(8,128)(2,1)S(1)} fusion(bf16[2048,4096]{1,0:T(8,128)(2,1)} %all-gather.4.cloned.1.call-done, bf16[2048,501]{0,1:T(8,128)(2,1)S(1)} %get-tuple-element.24, bf16[2048,501]{0,1:T(8,128)(2,1)S(1)} %get-tuple-element.23), kind=kOutput, calls=%fused_computation.4 | convolution fusion | flops 16823083008 | bytes 29089792 | tf_op jit(solution)/shard_map/dot_general | solution.py:43
  268.7 4.0 %fusion.8 = (bf16[4096,501]{0,1:T(8,128)(2,1)}, bf16[4096,501]{0,1:T(8,128)(2,1)}) fusion(bf16[4096,1002]{0,1:T(8,128)(2,1)S(1)} %convert_bitcast_fusion), kind=kLoop, calls=%fused_computation.34 | loop fusion | bytes 16416768 | tf_op jit(solution)/shard_map/slice | solution.py:83
  272.7 0.0 copy-done
  272.7 0.6 fusion.3
  (8 shorter events, 0.1 us)
Async XLA Ops:
  7.2 117.1 %all-gather.4.cloned.1.call-start = ((), (), s32[]{:S(2)}) async-start(), calls=%async_computation | async-start | bytes 17301504 | tf_op jit(solution)/shard_map/all_gather | solution.py:53
  139.0 103.3 %copy-start.1 = (f32[16]{0:T(128)S(1)}, f32[16]{0:T(128)}, u32[]{:S(2)}) copy-start(f32[16]{0:T(128)} %param.11) | copy-start | bytes 196
  243.6 29.1 %copy-start = (f32[8]{0:T(128)}, f32[8]{0:T(128)S(1)}, u32[]{:S(2)}) copy-start(f32[8]{0:T(128)S(1)} %get-tuple-element.18) | copy-start | bytes 100
Sparse Core Ops, SparseCore 0:
  33.8 90.3 all-gather.3
where the time goes:
time: 282 us
  blocking collectives  142 us (50%)
  waiting for transfers between devices  71.7 us (25%)
  matrix products  34.9 us (12%)
  between operations  15.9 us (6%)
  local copies, waits for them, and re-layouts  8.61 us (3%)
  other arithmetic  8.44 us (3%)
    all_gather x1, waiting for transfers between devices, shards(): whole_rows = lax.all_gather(token_rows, VOCAB, axis=1, tiled=True)  71.6 us
    psum x4, blocking collectives, by_axis_2(): shard = lax.psum(shard, axis)  60.1 us
    pmax x4, blocking collectives, by_axis(): shard = lax.pmax(shard, axis)  39.7 us
    all_gather x1, blocking collectives, shards(): seq_rows = lax.all_gather(hidden, 'ctx', axis=1, tiled=True)  26.5 us
    dot_general x1, matrix products, contract_rows(): lax.dot_general(block_rows, both_logits, (((0,), (0,)), ((), ())), prefer...  20.1 us
    all_gather x1, blocking collectives, gather_packed(): lines, at, finished = (lax.all_gather(flat, axis), 0, [])  16.1 us
    dot_general x1, matrix products, shards(): jnp.dot(whole_rows, head_weight, preferred_element_type=jnp.float32)  14.8 us
  transfers between devices with their start and end apart: 1, of which 1 were waited for; matrix products, arithmetic and copies ran while one was open for 1% of the time, Pallas kernels for 0%

commit v1 on v0

--- a/solution.py
+++ b/solution.py
@@ -9,6 +9,10 @@
 CTX_VOCAB = ("ctx", "vocab_0", "vocab_1", "vocab_2")
 strength = 0.1
 loss_scale = 256.0
+_do_halves = lambda u_in, peer_axis: jnp.concatenate(
+    lax.all_to_all(jnp.stack([u_in for _ in range(lax.axis_size(peer_axis))]), peer_axis, 0, 0),
+    axis=1,
+)
 
 
 def laid_out(pieces, dim):
@@ -50,7 +54,7 @@
     ids_all, mask_all = gather_packed((token_ids, response_mask), "ctx", (1, 1))
     token_rows = seq_rows.reshape(seq_rows.shape[0] * seq_rows.shape[1], seq_rows.shape[2])
     shard_width = head_weight.shape[1]
-    whole_rows = lax.all_gather(token_rows, VOCAB, axis=1, tiled=True)
+    whole_rows = _do_halves(token_rows, VOCAB)
     logits = jnp.dot(whole_rows, head_weight, preferred_element_type=jnp.float32)
     offset = lax.axis_index(CTX_VOCAB) * shard_width
     local_ids = ids_all.reshape(-1) - offset

time: 282 us -> 407 us (1.44)
  waiting for transfers between devices: 71.7 us -> 183 us
  starting transfers between devices: 0.04 us -> 14.1 us
  between operations: 15.9 us -> 2.58 us
  blocking collectives: 142 us -> 151 us
  local copies, waits for them, and re-layouts: 8.61 us -> 13.4 us
    all_to_all x0 -> x1, waiting for transfers between devices: none -> 183 us  [lax.all_to_all(jnp.stack([u_in for _ in range(lax.axis_size(peer_axis))])...]
    all_gather x1 -> x0, waiting for transfers between devices: 71.6 us -> none  [shards(): whole_rows = lax.all_gather(token_rows, VOCAB, axis=1, tiled=True)]
    all_to_all x0 -> x1, starting transfers between devices: none -> 14.1 us  [lax.all_to_all(jnp.stack([u_in for _ in range(lax.axis_size(peer_axis))])...]
    another operation x0 -> x2, local copies, waits for them, and re-layouts: none -> 6.2 us  [jnp.stack([u_in for _ in range(lax.axis_size(peer_axis))])]
    pmax x4, blocking collectives: 39.7 us -> 45.8 us  [by_axis(): shard = lax.pmax(shard, axis)]
  transfers between devices with their start and end apart: 1 -> 1, of which waited for: 1 -> 1; matrix products, arithmetic and copies ran while one was open for 1% -> 0% of each run, Pallas kernels for 0% -> 0%
where the time goes in v1:
time: 407 us
  waiting for transfers between devices  183 us (45%)
  blocking collectives  151 us (37%)
  matrix products  34.8 us (9%)
  starting transfers between devices  14.1 us (3%)
  local copies, waits for them, and re-layouts  13.4 us (3%)
  other arithmetic  7.71 us (2%)
    all_to_all x1, waiting for transfers between devices, lax.all_to_all(jnp.stack([u_in for _ in range(lax.axis_size(peer_axis))])...  183 us
    psum x4, blocking collectives, by_axis_2(): shard = lax.psum(shard, axis)  62.8 us
    pmax x4, blocking collectives, by_axis(): shard = lax.pmax(shard, axis)  45.8 us
    all_gather x1, blocking collectives, shards(): seq_rows = lax.all_gather(hidden, 'ctx', axis=1, tiled=True)  23.9 us
    dot_general x1, matrix products, contract_rows(): lax.dot_general(block_rows, both_logits, (((0,), (0,)), ((), ())), prefer...  20.1 us
    all_gather x1, blocking collectives, gather_packed(): lines, at, finished = (lax.all_gather(flat, axis), 0, [])  18.6 us
    dot_general x1, matrix products, shards(): jnp.dot(whole_rows, head_weight, preferred_element_type=jnp.float32)  14.7 us
    all_to_all x1, starting transfers between devices, lax.all_to_all(jnp.stack([u_in for _ in range(lax.axis_size(peer_axis))])...  14.1 us
  transfers between devices with their start and end apart: 1, of which 1 were waited for; matrix products, arithmetic and copies ran while one was open for 0% of the time, Pallas kernels for 0%

profile of v1, /device:TPU:1, one launch (start us, length us, event | category | flops | bytes accessed | tf_op | source)
XLA Modules:
  0.0 406.6 jit_solution(15621872713579685416)
XLA Ops:
  0.6 23.9 %all_gather.11 = bf16[16,128,128]{2,1,0:T(8,128)(2,1)S(1)} all-gather(bf16[16,16,128]{2,1,0:T(8,128)(2,1)} %param.6), channel_id=1, replica_groups=mesh['ctx'=8,'vocab_0'=4,'vocab_1'=4,'vocab_2'=2] {'ctx'}, dimensions={1}, use_global_device_ids=true | all-gather | bytes 589824 | tf_op jit(solution)/shard_map/all_gather | solution.py:53
  24.6 0.2 copy.18
  24.8 6.0 %stack.3 = bf16[32,2048,128]{1,2,0:T(8,128)(2,1)} broadcast(bf16[2048,128]{0,1:T(8,128)(2,1)S(1)} %copy.18), dimensions={1,2} | broadcast | bytes 17301504 | tf_op jit(solution)/shard_map/stack | solution.py:13
  30.8 0.0 copy-start
  30.8 0.0 copy-start.1
  30.8 0.0 copy-start.2
  30.8 14.1 %all-to-all-start = ((bf16[32,2048,128]{1,2,0:T(8,128)(2,1)}), bf16[32,2048,128]{1,2,0:T(8,128)(2,1)}, u32[]{:S(2)}, u32[]{:S(2)}) async-start(bf16[32,2048,128]{1,2,0:T(8,128)(2,1)} %stack.3), calls=%async_computation | async-start | bytes 33554432 | tf_op jit(solution)/shard_map/all_to_all | solution.py:13
  45.0 0.0 copy-done
  45.0 0.1 reshape.65
  45.0 0.0 copy-done.1
  45.0 0.1 reshape.66
  45.1 18.6 %all-gather.1 = s32[8,1,512]{2,1,0:T(1,128)S(1)} all-gather(s32[1,1,512]{2,1,0:T(1,128)S(1)} %bitcast.24), channel_id=2, replica_groups=mesh['ctx'=8,'vocab_0'=4,'vocab_1'=4,'vocab_2'=2] {'ctx'}, dimensions={0}, use_global_device_ids=true | all-gather | bytes 18432 | tf_op jit(solution)/shard_map/all_gather | solution.py:26
  63.7 0.1 sub.49
  63.9 0.1 sub.51
  63.9 0.1 convert_element_type.33
  64.1 0.1 convert_element_type.35
  64.1 0.0 copy-done.2
  64.1 0.1 compare_select_fusion.1
  64.2 182.8 %all-to-all-done = bf16[32,2048,128]{1,2,0:T(8,128)(2,1)} async-done(((bf16[32,2048,128]{1,2,0:T(8,128)(2,1)}), bf16[32,2048,128]{1,2,0:T(8,128)(2,1)}, u32[]{:S(2)}, u32[]{:S(2)}) %all-to-all-start) | async-done | bytes 16777248 | tf_op jit(solution)/shard_map/all_to_all | solution.py:13
  247.0 14.7 %fusion.9 = (f32[2048]{0:T(1024)S(1)}, f32[2048,501]{0,1:T(8,128)}) fusion(bf16[2048,4096]{0,1:T(8,128)(2,1)} %bitcast.4, bf16[4096,501]{0,1:T(8,128)(2,1)} %param.7), kind=kOutput, calls=%fused_computation.35 | convolution fusion | flops 8406409216 | bytes 24993792 | tf_op jit(solution)/shard_map/dot_general | solution.py:58
  261.7 0.0 copy-start.4
  261.7 12.7 %pmax.28 = f32[2048]{0:T(1024)S(1)} all-reduce(f32[2048]{0:T(1024)S(1)} %get-tuple-element.29), channel_id=1, replica_groups=mesh['ctx'=8,'vocab_0'=4,'vocab_1'=4,'vocab_2'=2] {'ctx'}, use_global_device_ids=true, to_apply=%region_6.0 | all-reduce | flops 2048 | bytes 16384 | tf_op jit(solution)/shard_map/pmax | solution.py:36
  274.5 6.1 %pmax.29 = f32[2048]{0:T(1024)S(1)} all-reduce(f32[2048]{0:T(1024)S(1)} %pmax.28), channel_id=1, replica_groups=mesh['ctx'=8,'vocab_0'=4,'vocab_1'=4,'vocab_2'=2] {'vocab_0'}, use_global_device_ids=true, to_apply=%region_7.0 | all-reduce | flops 2048 | bytes 16384 | tf_op jit(solution)/shard_map/pmax | solution.py:36
  280.6 18.0 %pmax.30 = f32[2048]{0:T(1024)S(1)} all-reduce(f32[2048]{0:T(1024)S(1)} %pmax.29), channel_id=1, replica_groups=mesh['ctx'=8,'vocab_0'=4,'vocab_1'=4,'vocab_2'=2] {'vocab_1'}, use_global_device_ids=true, to_apply=%region_8.0 | all-reduce | flops 2048 | bytes 16384 | tf_op jit(solution)/shard_map/pmax | solution.py:36
  298.6 9.0 %pmax.31 = f32[2048]{0:T(1024)S(1)} all-reduce(f32[2048]{0:T(1024)S(1)} %pmax.30), channel_id=1, replica_groups=mesh['ctx'=8,'vocab_0'=4,'vocab_1'=4,'vocab_2'=2] {'vocab_2'}, use_global_device_ids=true, to_apply=%region_9.0 | all-reduce | flops 2048 | bytes 16384 | tf_op jit(solution)/shard_map/pmax | solution.py:36
  307.6 3.3 exponential_reduce_fusion
  310.8 20.1 %all-reduce = (f32[2048]{0:T(1024)S(1)}, f32[2048]{0:T(1024)S(1)}) all-reduce(f32[2048]{0:T(1024)S(1)} %get-tuple-element.5, f32[2048]{0:T(1024)S(1)} %get-tuple-element.4), channel_id=1, replica_groups=mesh['ctx'=8,'vocab_0'=4,'vocab_1'=4,'vocab_2'=2] {'ctx'}, use_global_device_ids=true, to_apply=%region_1.0 | all-reduce | flops 4096 | bytes 32768 | tf_op jit(solution)/shard_map/psum | solution.py:42
  330.9 12.4 %all-reduce.2 = (f32[2048]{0:T(1024)S(1)}, f32[2048]{0:T(1024)S(1)}) all-reduce(f32[2048]{0:T(1024)S(1)} %get-tuple-element.6, f32[2048]{0:T(1024)S(1)} %get-tuple-element.7), channel_id=1, replica_groups=mesh['ctx'=8,'vocab_0'=4,'vocab_1'=4,'vocab_2'=2] {'vocab_0'}, use_global_device_ids=true, to_apply=%region_2.0 | all-reduce | flops 4096 | bytes 32768 | tf_op jit(solution)/shard_map/psum | solution.py:42
  343.3 12.4 %all-reduce.1 = (f32[2048]{0:T(1024)S(1)}, f32[2048]{0:T(1024)S(1)}) all-reduce(f32[2048]{0:T(1024)S(1)} %get-tuple-element.10, f32[2048]{0:T(1024)S(1)} %get-tuple-element.11), channel_id=1, replica_groups=mesh['ctx'=8,'vocab_0'=4,'vocab_1'=4,'vocab_2'=2] {'vocab_1'}, use_global_device_ids=true, to_apply=%region_3.0 | all-reduce | flops 4096 | bytes 32768 | tf_op jit(solution)/shard_map/psum | solution.py:42
  355.7 17.9 %all-reduce.3 = (f32[2048]{0:T(1024)S(1)}, f32[2048]{0:T(1024)S(1)}) all-reduce(f32[2048]{0:T(1024)S(1)} %get-tuple-element.8, f32[2048]{0:T(1024)S(1)} %get-tuple-element.9), channel_id=1, replica_groups=mesh['ctx'=8,'vocab_0'=4,'vocab_1'=4,'vocab_2'=2] {'vocab_2'}, use_global_device_ids=true, to_apply=%region_4.0 | all-reduce | flops 4096 | bytes 32768 | tf_op jit(solution)/shard_map/psum | solution.py:42
  373.7 0.1 bitcast_reduce_fusion
  373.8 0.0 copy-done.4
  373.8 0.6 gather_fusion.1
  374.4 0.6 gather_fusion
  375.1 0.0 copy-start.3
  375.1 0.6 scatter_custom_fusion
  375.7 0.8 scatter_fusion
  376.5 0.1 broadcast_multiply_fusion
  376.6 3.5 multiply_convert_fusion.1
  380.1 20.1 %convert_bitcast_fusion = bf16[4096,1002]{0,1:T(8,128)(2,1)S(1)} fusion(bf16[2048,4096]{0,1:T(8,128)(2,1)} %bitcast.4, bf16[2048,501]{0,1:T(8,128)(2,1)S(1)} %get-tuple-element.24, bf16[2048,501]{0,1:T(8,128)(2,1)S(1)} %get-tuple-element.23), kind=kOutput, calls=%fused_computation.4 | convolution fusion | flops 16823083008 | bytes 29089792 | tf_op jit(solution)/shard_map/dot_general | solution.py:47
  400.2 4.0 fusion.8
  404.2 0.0 copy-done.3
  404.3 0.6 fusion.3
  (8 shorter events, 0.1 us)
Async XLA Ops:
  30.8 14.2 %copy-start = (s32[16,16]{1,0:T(8,128)S(1)}, s32[16,16]{1,0:T(8,128)}, u32[]{:S(2)}) copy-start(s32[16,16]{1,0:T(8,128)} %param.8) | copy-start | bytes 3076
  30.8 14.3 %copy-start.1 = (s32[16,16]{1,0:T(8,128)S(1)}, s32[16,16]{1,0:T(8,128)}, u32[]{:S(2)}) copy-start(s32[16,16]{1,0:T(8,128)} %param.9) | copy-start | bytes 3076
  30.8 33.4 %copy-start.2 = (s32[16]{0:T(128)S(1)}, s32[16]{0:T(128)}, u32[]{:S(2)}) copy-start(s32[16]{0:T(128)} %param.10) | copy-start | bytes 196
  30.8 216.2 %all-to-all-start = ((bf16[32,2048,128]{1,2,0:T(8,128)(2,1)}), bf16[32,2048,128]{1,2,0:T(8,128)(2,1)}, u32[]{:S(2)}, u32[]{:S(2)}) async-start(bf16[32,2048,128]{1,2,0:T(8,128)(2,1)} %stack.3), calls=%async_computation | async-start | bytes 33554432 | tf_op jit(solution)/shard_map/all_to_all | solution.py:13
  261.7 112.0 %copy-start.4 = (f32[16]{0:T(128)S(1)}, f32[16]{0:T(128)}, u32[]{:S(2)}) copy-start(f32[16]{0:T(128)} %param.11) | copy-start | bytes 196
  375.1 29.2 %copy-start.3 = (f32[8]{0:T(128)}, f32[8]{0:T(128)S(1)}, u32[]{:S(2)}) copy-start(f32[8]{0:T(128)S(1)} %get-tuple-element.18) | copy-start | bytes 100
